TPU v7x, 32 devices: a whole 2x2x4 slice. The times are simulated.
32 devices in a mesh: rep: 4 (over z), fsdp: 2 (over x), tp: 4 (over y, core).
Axes of the slice: x: 2, y: 2, z: 4, core: 2. Of those that a mesh axis runs over, the one named last changes fastest.
Arguments:
- gate_pre: bfloat16 [1024, 14848], P(('rep', 'fsdp'), 'tp'), may hold values from -6 to 6
- up_pre: bfloat16 [1024, 14848], P(('rep', 'fsdp'), 'tp'), may hold values from -30 to 30
- out_grad: bfloat16 [1024, 4096], P(('rep', 'fsdp')), may hold values from -30 to 30
Outputs:
- down_grad: bfloat16 [4096, 14848], P('fsdp', 'tp')
All inputs are finite; a program needn't handle non-finite values.
Results may differ from a plain program's by a relative error of at most 0.02.
Values may be sent and summed in bfloat16 or wider, within the bound.
A program may use at most 128 MiB of HBM per device.

v0:
```python
import jax
import jax.numpy as jnp
from jax import lax
from jax.sharding import PartitionSpec as P


def on_device(gate_pre, up_pre, out_grad):
    hidden = (jax.nn.silu(gate_pre.astype(jnp.float32)) * up_pre.astype(jnp.float32)).astype(
        jnp.bfloat16
    )
    feature_rows = out_grad.shape[1] // lax.axis_size("fsdp")
    block_rows = out_grad.shape[0]
    spread = lax.all_to_all(out_grad, "fsdp", split_axis=1, concat_axis=0, tiled=True)

    def advance(running, paired):
        grad_rows, hidden_rows = paired
        partial_term = jnp.dot(grad_rows.T, hidden_rows, preferred_element_type=jnp.float32)
        return (running + partial_term.astype(jnp.bfloat16).astype(jnp.float32), None)

    starting = jnp.zeros((feature_rows, hidden.shape[1]), jnp.float32)
    running = starting
    portion = lax.all_gather(hidden, "fsdp", axis=0, tiled=True)
    row_count = portion.shape[0]
    blocks = row_count // block_rows
    grad_rows = spread
    running, unused = lax.scan(
        advance,
        running,
        (
            grad_rows.reshape(blocks, block_rows, grad_rows.shape[1]),
            portion.reshape(blocks, block_rows, portion.shape[1]),
        ),
    )
    summed = lax.psum(running.astype(jnp.bfloat16), "rep").astype(jnp.float32)
    square_total = lax.psum(jnp.sum(summed * summed), ("fsdp", "tp"))
    entry_count = summed.shape[0] * lax.axis_size("fsdp") * summed.shape[1] * lax.axis_size("tp")
    factor = 1.0 / jnp.sqrt(square_total / entry_count + 1e-06)
    return (summed * factor).astype(jnp.bfloat16)


def solution(mesh):
    return jax.shard_map(
        on_device,
        mesh=mesh,
        in_specs=(P(("rep", "fsdp"), "tp"), P(("rep", "fsdp"), "tp"), P(("rep", "fsdp"), None)),
        out_specs=P("fsdp", "tp"),
        check_vma=False,
    )
```

profile of v0, /device:TPU:0, one launch (start us, length us, event | category | flops | bytes accessed | tf_op | source)
XLA Modules:
  0.0 660.7 jit_solution(3080684873038719467)
XLA Ops:
  6.5 0.0 all-gather.2.cloned.1.call-start
  6.5 3.0 fusion.11
  9.5 0.0 all-gather.2.cloned.1.call-update
  9.6 2.3 copy.4
  11.8 4.2 all-to-all-start
  16.1 0.0 all-reduce.2.cloned.1.call-start
  16.1 23.0 %all-to-all-done = bf16[128,2,2048]{0,2,1:T(8,128)(2,1)S(1)} async-done(((bf16[128,2,2048]{0,2,1:T(8,128)(2,1)}), bf16[128,2,2048]{0,2,1:T(8,128)(2,1)S(1)}, u32[]{:S(2)}, u32[]{:S(2)}) %all-to-all-start) | async-done | bytes 1048608 | tf_op jit(solution)/shard_map/all_to_all | solution.py:13
  39.1 12.0 %all-gather.2.cloned.1.call-done = bf16[256,3712]{1,0:T(8,128)(2,1)} async-done(((bf16[128,3712]{1,0:T(8,128)(2,1)}), bf16[256,3712]{1,0:T(8,128)(2,1)}) %all-gather.2.cloned.1.call-update) | async-done | bytes 1900560 | tf_op jit(solution)/shard_map/all_gather | solution.py:22
  51.1 35.5 %while.11 = (s32[]{:T(128)}, f32[2048,3712]{1,0:T(8,128)}, bf16[2,128,2048]{1,2,0:T(8,128)(2,1)S(1)}, bf16[2,128,3712]{2,1,0:T(8,128)(2,1)}, s32[]{:T(128)}, /*index=5*/s32[]{:T(128)}) while((s32[]{:T(128)}, f32[2048,3712]{1,0:T(8,128)}, bf16[2,128,2048]{1,2,0:T(8,128)(2,1)S(1)}, bf16[2,128,3712]{2,1,0:T(8,128)(2,1)}, s32[]{:T(128)}, ...), condition=%wide.region_1.2_spmd.clone, body=%wide.region_0.1_spmd.clone.sunk | while | flops 1976565760 | bytes 62293588 | solution.py:26
  51.1 12.6 %select_add_fusion.2 = f32[2048,3712]{1,0:T(8,128)} fusion(f32[2048,3712]{1,0:T(8,128)} %get-tuple-element.87, pred[]{:T(512)S(6)} %compare.3, bf16[2,128,3712]{2,1,0:T(8,128)(2,1)} %get-tuple-element.95, s32[]{:T(128)S(6)} %copy.9, bf16[2,128,2048]{1,2,0:T(8,128)(2,1)S(1)} %get-tuple-element.94), kind=kOutput, calls=%fused_computation.clone.1 | convolution fusion | flops 1976565760 | bytes 62293504 | tf_op jit(solution)/shard_map/while/body/eval_jaxpr/dot_general | solution.py:17
  63.7 22.9 %select_add_fusion.2 = f32[2048,3712]{1,0:T(8,128)} fusion(f32[2048,3712]{1,0:T(8,128)} %get-tuple-element.87, pred[]{:T(512)S(6)} %compare.3, bf16[2,128,3712]{2,1,0:T(8,128)(2,1)} %get-tuple-element.95, s32[]{:T(128)S(6)} %copy.9, bf16[2,128,2048]{1,2,0:T(8,128)(2,1)S(1)} %get-tuple-element.94), kind=kOutput, calls=%fused_computation.clone.1 | convolution fusion | flops 1976565760 | bytes 62293504 | tf_op jit(solution)/shard_map/while/body/eval_jaxpr/dot_general | solution.py:17
  86.6 15.9 %convert_element_type.27 = bf16[2048,3712]{1,0:T(8,128)(2,1)} convert(f32[2048,3712]{1,0:T(8,128)} %get-tuple-element.27) | non-fusion elementwise | flops 7602176 | bytes 45613056 | tf_op jit(solution)/shard_map/convert_element_type | solution.py:34
  102.5 0.0 all-reduce.2.cloned.1.call-update
  102.6 511.4 %all-reduce.2.cloned.1.call-done = bf16[2048,3712]{1,0:T(8,128)(2,1)} async-done(((bf16[2048,3712]{1,0:T(8,128)(2,1)}), bf16[2048,3712]{1,0:T(8,128)(2,1)}) %all-reduce.2.cloned.1.call-update) | async-done | bytes 15204368 | tf_op jit(solution)/shard_map/psum | solution.py:34
  614.0 13.7 %fusion.5 = f32[]{:T(128)} fusion(bf16[2048,3712]{1,0:T(8,128)(2,1)} %all-reduce.2.cloned.1.call-done), kind=kLoop, calls=%fused_computation.8 | loop fusion | flops 22806528 | bytes 15204356 | tf_op jit(solution)/shard_map/reduce_sum | solution.py:35
  627.7 14.1 %psum.15 = f32[]{:T(128)} all-reduce(f32[]{:T(128)} %fusion.5), channel_id=1, replica_groups=mesh['rep'=4,'fsdp'=2,'tp'=4] {'fsdp','tp'}, use_global_device_ids=true, to_apply=%region_4.5 | all-reduce | flops 1 | bytes 8 | tf_op jit(solution)/shard_map/psum | solution.py:35
  642.5 11.4 %fusion.6 = bf16[2048,3712]{1,0:T(8,128)(2,1)} fusion(bf16[2048,3712]{1,0:T(8,128)(2,1)} %all-reduce.2.cloned.1.call-done, f32[]{:T(128)S(6)} %sqrt.3), kind=kLoop, calls=%fused_computation.9 | loop fusion | flops 22806528 | bytes 30408708 | tf_op jit(solution)/shard_map/convert_element_type | solution.py:38
  (1 shorter events, 0.0 us)
Async XLA Ops:
  6.5 44.6 %all-gather.2.cloned.1.call-start = ((), (), s32[]{:S(2)}) async-start(), calls=%async_computation.1 | async-start | bytes 2850816 | tf_op jit(solution)/shard_map/all_gather | solution.py:22
  11.8 27.3 %all-to-all-start = ((bf16[128,2,2048]{0,2,1:T(8,128)(2,1)}), bf16[128,2,2048]{0,2,1:T(8,128)(2,1)S(1)}, u32[]{:S(2)}, u32[]{:S(2)}) async-start(bf16[128,2,2048]{0,2,1:T(8,128)(2,1)} %bitcast), calls=%async_computation | async-start | bytes 2097152 | tf_op jit(solution)/shard_map/all_to_all | solution.py:13
  16.1 597.9 %all-reduce.2.cloned.1.call-start = ((), (), s32[]{:S(2)}) async-start(), calls=%async_computation.2 | async-start | bytes 30408704 | tf_op jit(solution)/shard_map/psum | solution.py:34
Sparse Core Ops, SparseCore 0:
  9.7 41.3 all-gather.1
  102.7 511.2 all-reduce.1
where the time goes:
time: 661 us
  waiting for transfers between devices  546 us (83%)
  other arithmetic  44.1 us (7%)
  matrix products  35.5 us (5%)
  blocking collectives  14.1 us (2%)
  between operations  14.1 us (2%)
    psum x1, waiting for transfers between devices, on_device(): summed = lax.psum(running.astype(jnp.bfloat16), 'rep').astype(jnp.float32)  511 us
    dot_general x2, matrix products, advance(): jnp.dot(grad_rows.T, hidden_rows, preferred_element_type=jnp.float32)  35.5 us
    all_to_all x1, waiting for transfers between devices, on_device(): lax.all_to_all(out_grad, 'fsdp', split_axis=1, concat_axis=0, tiled=True)  23 us
    convert_element_type x1, other arithmetic, on_device(): summed = lax.psum(running.astype(jnp.bfloat16), 'rep').astype(jnp.float32)  15.9 us
    psum x1, blocking collectives, on_device(): square_total = lax.psum(jnp.sum(summed * summed), ('fsdp', 'tp'))  14.1 us
    reduce_sum x1, other arithmetic, on_device(): square_total = lax.psum(jnp.sum(summed * summed), ('fsdp', 'tp'))  13.7 us
  transfers between devices with their start and end apart: 3, of which 3 were waited for; matrix products, arithmetic and copies ran while one was open for 0% of the time, Pallas kernels for 0%

commit v1 on v0

--- a/solution.py
+++ b/solution.py
@@ -31,7 +31,9 @@
             portion.reshape(blocks, block_rows, portion.shape[1]),
         ),
     )
-    summed = lax.psum(running.astype(jnp.bfloat16), "rep").astype(jnp.float32)
+    summed = jnp.sum(lax.all_gather(running.astype(jnp.bfloat16), "rep"), axis=0).astype(
+        jnp.float32
+    )
     square_total = lax.psum(jnp.sum(summed * summed), ("fsdp", "tp"))
     entry_count = summed.shape[0] * lax.axis_size("fsdp") * summed.shape[1] * lax.axis_size("tp")
     factor = 1.0 / jnp.sqrt(square_total / entry_count + 1e-06)

time: 661 us -> 1190 us (1.80)
  waiting for transfers between devices: 546 us -> 1040 us
  other arithmetic: 44.1 us -> 72.6 us
    all_gather x0 -> x1, waiting for transfers between devices: none -> 1010 us  [on_device(): lax.all_gather(running.astype(jnp.bfloat16), 'rep')]
    psum x1 -> x0, waiting for transfers between devices: 511 us -> none  [on_device(): summed = lax.psum(running.astype(jnp.bfloat16), 'rep').astype(jnp.float32)]
    reduce_sum x0 -> x1, other arithmetic: none -> 28.5 us  [on_device(): jnp.sum(lax.all_gather(running.astype(jnp.bfloat16), 'rep'), axis=0)]
where the time goes in v1:
time: 1190 us
  waiting for transfers between devices  1040 us (87%)
  other arithmetic  72.6 us (6%)
  matrix products  35.5 us (3%)
  blocking collectives  14.4 us (1%)
  between operations  14 us (1%)
    all_gather x1, waiting for transfers between devices, on_device(): lax.all_gather(running.astype(jnp.bfloat16), 'rep')  1010 us
    dot_general x2, matrix products, advance(): jnp.dot(grad_rows.T, hidden_rows, preferred_element_type=jnp.float32)  35.5 us
    reduce_sum x1, other arithmetic, on_device(): jnp.sum(lax.all_gather(running.astype(jnp.bfloat16), 'rep'), axis=0)  28.5 us
  transfers between devices with their start and end apart: 3, of which 3 were waited for; matrix products, arithmetic and copies ran while one was open for 0% of the time, Pallas kernels for 0%

profile of v1, /device:TPU:0, one launch (start us, length us, event | category | flops | bytes accessed | tf_op | source)
XLA Modules:
  0.0 1187.1 jit_solution(812235288750005157)
XLA Ops:
  6.5 0.0 all-gather.4.cloned.1.call-start
  6.5 3.0 fusion.11
  9.5 0.0 all-gather.4.cloned.1.call-update
  9.6 2.3 copy.4
  11.8 4.2 all-to-all-start
  16.1 0.0 all-gather.6.cloned.1.call-start
  16.1 23.0 %all-to-all-done = bf16[128,2,2048]{0,2,1:T(8,128)(2,1)S(1)} async-done(((bf16[128,2,2048]{0,2,1:T(8,128)(2,1)}), bf16[128,2,2048]{0,2,1:T(8,128)(2,1)S(1)}, u32[]{:S(2)}, u32[]{:S(2)}) %all-to-all-start) | async-done | bytes 1048608 | tf_op jit(solution)/shard_map/all_to_all | solution.py:13
  39.1 12.0 %all-gather.4.cloned.1.call-done = bf16[256,3712]{1,0:T(8,128)(2,1)} async-done(((bf16[128,3712]{1,0:T(8,128)(2,1)}), bf16[256,3712]{1,0:T(8,128)(2,1)}) %all-gather.4.cloned.1.call-update) | async-done | bytes 1900560 | tf_op jit(solution)/shard_map/all_gather | solution.py:22
  51.1 35.5 %while.11 = (s32[]{:T(128)}, f32[2048,3712]{1,0:T(8,128)}, bf16[2,128,2048]{1,2,0:T(8,128)(2,1)S(1)}, bf16[2,128,3712]{2,1,0:T(8,128)(2,1)}, s32[]{:T(128)}, /*index=5*/s32[]{:T(128)}) while((s32[]{:T(128)}, f32[2048,3712]{1,0:T(8,128)}, bf16[2,128,2048]{1,2,0:T(8,128)(2,1)S(1)}, bf16[2,128,3712]{2,1,0:T(8,128)(2,1)}, s32[]{:T(128)}, ...), condition=%wide.region_1.2_spmd.clone, body=%wide.region_0.1_spmd.clone.sunk | while | flops 1976565760 | bytes 62293588 | solution.py:26
  51.1 12.6 %select_add_fusion.2 = f32[2048,3712]{1,0:T(8,128)} fusion(f32[2048,3712]{1,0:T(8,128)} %get-tuple-element.87, pred[]{:T(512)S(6)} %compare.3, bf16[2,128,3712]{2,1,0:T(8,128)(2,1)} %get-tuple-element.95, s32[]{:T(128)S(6)} %copy.9, bf16[2,128,2048]{1,2,0:T(8,128)(2,1)S(1)} %get-tuple-element.94), kind=kOutput, calls=%fused_computation.clone.1 | convolution fusion | flops 1976565760 | bytes 62293504 | tf_op jit(solution)/shard_map/while/body/eval_jaxpr/dot_general | solution.py:17
  63.7 22.9 %select_add_fusion.2 = f32[2048,3712]{1,0:T(8,128)} fusion(f32[2048,3712]{1,0:T(8,128)} %get-tuple-element.87, pred[]{:T(512)S(6)} %compare.3, bf16[2,128,3712]{2,1,0:T(8,128)(2,1)} %get-tuple-element.95, s32[]{:T(128)S(6)} %copy.9, bf16[2,128,2048]{1,2,0:T(8,128)(2,1)S(1)} %get-tuple-element.94), kind=kOutput, calls=%fused_computation.clone.1 | convolution fusion | flops 1976565760 | bytes 62293504 | tf_op jit(solution)/shard_map/while/body/eval_jaxpr/dot_general | solution.py:17
  86.6 15.9 %convert_element_type.29 = bf16[2048,3712]{1,0:T(8,128)(2,1)} convert(f32[2048,3712]{1,0:T(8,128)} %get-tuple-element.27) | non-fusion elementwise | flops 7602176 | bytes 45613056 | tf_op jit(solution)/shard_map/convert_element_type | solution.py:34
  102.5 0.0 all-gather.6.cloned.1.call-update
  102.6 1009.1 %all-gather.6.cloned.1.call-done = bf16[8192,3712]{1,0:T(8,128)(2,1)} async-done(((bf16[2048,3712]{1,0:T(8,128)(2,1)}), bf16[8192,3712]{1,0:T(8,128)(2,1)}) %all-gather.6.cloned.1.call-update) | async-done | bytes 60817424 | tf_op jit(solution)/shard_map/all_gather | solution.py:34
  1111.7 28.5 %reduce_sum.21 = bf16[2048,3712]{1,0:T(8,128)(2,1)} reduce(bf16[4,2048,3712]{2,1,0:T(8,128)(2,1)} %bitcast.15, bf16[]{:T(256)} %constant.22.clone.1), dimensions={0}, to_apply=%region_2.3 | reduce | flops 22806528 | bytes 76021760 | tf_op jit(solution)/shard_map/reduce_sum | solution.py:34
  1140.1 13.7 %fusion.5 = f32[]{:T(128)} fusion(bf16[2048,3712]{1,0:T(8,128)(2,1)} %reduce_sum.21), kind=kLoop, calls=%fused_computation.8 | loop fusion | flops 22806528 | bytes 15204356 | tf_op jit(solution)/shard_map/reduce_sum | solution.py:37
  1153.9 14.4 %psum.7 = f32[]{:T(128)} all-reduce(f32[]{:T(128)} %fusion.5), channel_id=1, replica_groups=mesh['rep'=4,'fsdp'=2,'tp'=4] {'fsdp','tp'}, use_global_device_ids=true, to_apply=%region_4.5 | all-reduce | flops 1 | bytes 8 | tf_op jit(solution)/shard_map/psum | solution.py:37
  1168.9 11.4 fusion.6
  (1 shorter events, 0.0 us)
Async XLA Ops:
  6.5 44.6 %all-gather.4.cloned.1.call-start = ((), (), s32[]{:S(2)}) async-start(), calls=%async_computation.1 | async-start | bytes 2850816 | tf_op jit(solution)/shard_map/all_gather | solution.py:22
  11.8 27.3 %all-to-all-start = ((bf16[128,2,2048]{0,2,1:T(8,128)(2,1)}), bf16[128,2,2048]{0,2,1:T(8,128)(2,1)S(1)}, u32[]{:S(2)}, u32[]{:S(2)}) async-start(bf16[128,2,2048]{0,2,1:T(8,128)(2,1)} %bitcast), calls=%async_computation | async-start | bytes 2097152 | tf_op jit(solution)/shard_map/all_to_all | solution.py:13
  16.1 1095.6 %all-gather.6.cloned.1.call-start = ((), (), s32[]{:S(2)}) async-start(), calls=%async_computation.2 | async-start | bytes 76021760 | tf_op jit(solution)/shard_map/all_gather | solution.py:34
Sparse Core Ops, SparseCore 0:
  9.7 41.3 all-gather.3
  102.7 1008.9 all-gather.5
